TPU v7x, 512 devices: a whole 4x4x16 slice. The times are simulated.
512 devices in a mesh: row: 32 (over z_lo, x), col: 16 (over z_hi, y, core).
Axes of the slice: x: 4, y: 4, z: 16 (z_hi: 2, z_lo: 8; z = z_hi * 8 + z_lo), core: 2. Of those that a mesh axis runs over, the one named last changes fastest.
Arguments:
- noisy: float32 [1024, 32768], P('row', 'col'), may hold values from -9 to 9
Outputs:
- denoised: float32 [1024, 32768], P('row', 'col')
- gap: float32 [4], replicated
All inputs are finite; a program needn't handle non-finite values.
Results may differ from a plain program's by a relative error of at most 0.0003.
Values sent between devices are 32-bit elements; how exact they have to be, the bound alone decides.
A program may use at most 64 MiB of HBM per device.

v0:
```python
import jax
import jax.numpy as jnp
from jax import lax
from jax.sharding import Mesh
from jax.sharding import PartitionSpec as P

ITERS = 4
ROW = ("row_0", "row_1")
COL = ("col_0", "col_1", "col_2")
ROW_COL = ("row_0", "row_1", "col_0", "col_1", "col_2")
fidelity = 8.0
primal_step = 0.35
dual_step = 0.35


def with_halo(shard, sides, width):
    for axis, dim in sides:
        size, length = (lax.axis_size(axis), shard.shape[dim])
        up = [(i, (i + 1) % size) for i in range(size - 1)]
        down = [(j, i) for i, j in up]
        last = lax.slice_in_dim(shard, length - width, length, axis=dim)
        first = lax.slice_in_dim(shard, 0, width, axis=dim)
        before = lax.ppermute(last, axis, up)
        after = lax.ppermute(first, axis, down)
        shard = jnp.concatenate([before, shard, after], axis=dim)
    return shard


def by_axis(shard, axes):
    for axis in axes:
        shard = lax.psum(shard, axis)
    return shard


def gap_piece(edge_rows, edge_cols, primal, noisy, diverged):
    return jnp.sum(jnp.sqrt(edge_rows * edge_rows + edge_cols * edge_cols)) + jnp.sum(
        0.5 * fidelity * (primal - noisy) ** 2
        + noisy * diverged
        + diverged * diverged / (2.0 * fidelity)
    )


def deep_run(noisy):
    tile_rows, tile_cols = noisy.shape
    rows_all = lax.axis_size(ROW) * tile_rows
    cols_all = lax.axis_size(COL) * tile_cols
    margin = ITERS + 1
    framed = with_halo(noisy, ((ROW, 0), (COL, 1)), margin)
    global_rows = (
        lax.axis_index(ROW) * tile_rows
        - margin
        + jnp.arange(tile_rows + 2 * margin, dtype=jnp.int32)
    )
    global_cols = (
        lax.axis_index(COL) * tile_cols
        - margin
        + jnp.arange(tile_cols + 2 * margin, dtype=jnp.int32)
    )
    rows_inside = (global_rows >= 0) & (global_rows < rows_all)
    rows_inner = (global_rows >= 0) & (global_rows < rows_all - 1)
    cols_inside = (global_cols >= 0) & (global_cols < cols_all)
    cols_inner = (global_cols >= 0) & (global_cols < cols_all - 1)
    mask_rows = (rows_inner[:, None] & cols_inside[None, :]).astype(jnp.float32)
    mask_cols = (rows_inside[:, None] & cols_inner[None, :]).astype(jnp.float32)
    frame_rows, frame_cols = framed.shape

    def masked_grads(field):
        row_diff = jnp.concatenate(
            [field[1:] - field[:-1], jnp.zeros((1, frame_cols), jnp.float32)], 0
        )
        col_diff = jnp.concatenate(
            [field[:, 1:] - field[:, :-1], jnp.zeros((frame_rows, 1), jnp.float32)], 1
        )
        return (row_diff * mask_rows, col_diff * mask_cols)

    primal = framed
    previous = framed
    dual = jnp.zeros((2,) + framed.shape, jnp.float32)
    pieces = []
    for iteration in range(ITERS):
        extrapolated = 2.0 * primal - previous
        grad_rows, grad_cols = masked_grads(extrapolated)
        trial = dual + dual_step * jnp.stack([grad_rows, grad_cols])
        shrink = 1.0 / jnp.maximum(1.0, jnp.sqrt(trial[0] * trial[0] + trial[1] * trial[1]))
        dual = trial * shrink
        diverged = (
            dual[0]
            - jnp.concatenate([jnp.zeros((1, frame_cols), jnp.float32), dual[0, :-1]], 0)
            + dual[1]
            - jnp.concatenate([jnp.zeros((frame_rows, 1), jnp.float32), dual[1, :, :-1]], 1)
        )
        updated = (primal + primal_step * diverged + primal_step * fidelity * framed) / (
            1.0 + primal_step * fidelity
        )
        previous = primal
        primal = updated
        edge_rows, edge_cols = masked_grads(primal)
        owned_r = slice(margin, margin + tile_rows)
        owned_c = slice(margin, margin + tile_cols)
        pieces.append(
            gap_piece(
                edge_rows[owned_r, owned_c],
                edge_cols[owned_r, owned_c],
                primal[owned_r, owned_c],
                noisy,
                diverged[owned_r, owned_c],
            )
        )
    return (primal[margin : margin + tile_rows, margin : margin + tile_cols], pieces)


def on_device(noisy):
    cells = lax.axis_size(ROW) * noisy.shape[0] * lax.axis_size(COL) * noisy.shape[1]
    primal, pieces = deep_run(noisy)
    gap = by_axis(jnp.stack(pieces), ROW_COL) / cells
    return (primal, gap)


def solution(mesh):
    torus = Mesh(mesh.devices.reshape(8, 4, 2, 4, 2), ("row_0", "row_1", "col_0", "col_1", "col_2"))
    return jax.shard_map(
        on_device,
        mesh=torus,
        in_specs=(P(ROW, COL),),
        out_specs=(P(ROW, COL), P()),
        check_vma=False,
    )
```

profile of v0, /device:TPU:1, one launch (start us, length us, event | category | flops | bytes accessed | tf_op | source)
XLA Modules:
  0.0 118.6 jit_solution(13011369884884892752)
XLA Ops:
  0.6 0.9 fusion.92
  1.6 1.3 %collective-permute-start.1 = (f32[5,2048]{1,0:T(8,128)S(1)}, f32[5,2048]{1,0:T(8,128)S(1)}, u32[]{:S(2)}, u32[]{:S(2)}) collective-permute-start(f32[5,2048]{1,0:T(8,128)S(1)} %get-tuple-element.24), channel_id=1, source_target_pairs={{16,0},{32,16},{48,32},{64,48},{80,64},{96,80},{112,96},{128,112},... | collective-permute-start | bytes 122888 | tf_op jit(solution)/shard_map/ppermute | solution.py:24
  2.9 4.6 %collective-permute-start = (f32[5,2048]{1,0:T(8,128)S(1)}, f32[5,2048]{1,0:T(8,128)S(1)}, u32[]{:S(2)}, u32[]{:S(2)}) collective-permute-start(f32[5,2048]{1,0:T(8,128)S(1)} %get-tuple-element.23), channel_id=1, source_target_pairs={{0,16},{16,32},{32,48},{48,64},{64,80},{80,96},{96,112},{112,128},... | collective-permute-start | bytes 122888 | tf_op jit(solution)/shard_map/ppermute | solution.py:23
  7.5 0.1 broadcast_and_fusion
  7.6 1.1 collective-permute-done
  8.9 5.1 %collective-permute-start.2 = (f32[42,5]{1,0:T(8,128)S(1)}, f32[42,5]{1,0:T(8,128)S(1)}, u32[]{:S(2)}, u32[]{:S(2)}) collective-permute-start(f32[42,5]{1,0:T(8,128)S(1)} %get-tuple-element.22), channel_id=1, source_target_pairs={{0,1},{1,2},{2,3},{3,4},{4,5},{5,6},{6,7},{7,8},{8,9},{9,10},{10,1... | collective-permute-start | bytes 2528 | tf_op jit(solution)/shard_map/ppermute | solution.py:23
  14.0 5.5 %collective-permute-start.3 = (f32[42,5]{1,0:T(8,128)S(1)}, f32[42,5]{1,0:T(8,128)S(1)}, u32[]{:S(2)}, u32[]{:S(2)}) collective-permute-start(f32[42,5]{1,0:T(8,128)S(1)} %get-tuple-element.21), channel_id=1, source_target_pairs={{1,0},{2,1},{3,2},{4,3},{5,4},{6,5},{7,6},{8,7},{9,8},{10,9},{11,1... | collective-permute-start | bytes 2528 | tf_op jit(solution)/shard_map/ppermute | solution.py:24
  19.5 0.1 broadcast_and_fusion.1
  19.6 0.7 collective-permute-done.3
  20.3 0.3 concatenate.79
  20.6 0.2 slice_subtract_fusion.14
  20.8 0.1 fusion.9
  21.0 0.1 fusion.5
  21.2 0.2 fusion.45
  21.5 0.2 fusion.46
  21.9 0.2 slice_subtract_fusion.12
  22.1 0.1 fusion.10
  22.2 0.1 fusion.6
  22.3 0.1 fusion
  22.5 0.2 fusion.36
  22.6 0.2 broadcast_multiply_fusion.2
  22.9 0.3 multiply_subtract_fusion.2
  23.2 0.2 slice_subtract_fusion.10
  23.4 0.1 fusion.11
  23.6 0.1 fusion.7
  23.7 0.2 fusion.1
  23.9 0.2 fusion.28
  24.1 0.3 broadcast_multiply_fusion.1
  24.5 0.4 multiply_subtract_fusion.1
  24.8 0.2 slice_subtract_fusion.8
  25.1 0.1 fusion.12
  25.2 0.1 fusion.8
  25.3 0.3 fusion.2
  25.6 0.2 fusion.20
  25.8 0.4 broadcast_multiply_fusion
  26.3 0.2 slice_subtract_fusion.6
  26.5 0.2 slice_subtract_fusion.4
  26.7 0.3 add_multiply_fusion
  27.0 0.2 slice_subtract_fusion.2
  27.3 0.2 slice_subtract_fusion
  27.5 2.0 %fusion.76 = (f32[]{:T(128)}, f32[]{:T(128)}, f32[]{:T(128)}, f32[]{:T(128)}, f32[32,2048]{1,0:T(8,128)}) fusion(f32[32,2048]{1,0:T(8,128)S(1)} %copy-done, f32[42,2058]{1,0:T(8,128)S(1)} %get-tuple-element.11, f32[42,2058]{1,0:T(8,128)S(1)} %get-tuple-element.12, f32[42,2058]{1,0:T(8,128)S(1)} %get-tuple-element.20, f32[42,2058]{1,0:T(8,128)S(1)} %get-tuple-element.18, ...), kind=kLoop, calls=%fused_computation.149 | loop fusion | flops 2359292 | bytes 2621456 | tf_op jit(solution)/shard_map/reduce_sum | solution.py:36
  29.5 1.6 %fusion.80 = (f32[]{:T(128)}, f32[]{:T(128)}, f32[]{:T(128)}, f32[]{:T(128)}) fusion(f32[42,2057]{1,0:T(8,128)S(1)} %slice_subtract_fusion.6, f32[41,2058]{1,0:T(8,128)S(1)} %slice_subtract_fusion.7, pred[42,2058]{1,0:T(8,128)(4,1)S(1)} %broadcast_and_fusion, pred[42,2058]{1,0:T(8,128)(4,1)S(1)} %broadcast_and_fusion.1, ...), kind=kLoop, calls=%fused_computation.154 | loop fusion | flops 1572860 | bytes 2863440 | tf_op jit(solution)/shard_map/reduce_sum | solution.py:36
  36.3 36.1 %psum.35 = f32[4]{0:T(128)S(1)} all-reduce(f32[4]{0:T(128)S(1)} %pad_maximum_fusion.2), channel_id=1, replica_groups=mesh['row_0'=8,'row_1'=4,'col_0'=2,'col_1'=4,'col_2'=2] {'row_0'}, use_global_device_ids=true, to_apply=%region_8.0 | all-reduce | flops 4 | bytes 32 | tf_op jit(solution)/shard_map/psum | solution.py:31
  72.4 6.0 %psum.36 = f32[4]{0:T(128)S(1)} all-reduce(f32[4]{0:T(128)S(1)} %psum.35), channel_id=1, replica_groups=mesh['row_0'=8,'row_1'=4,'col_0'=2,'col_1'=4,'col_2'=2] {'row_1'}, use_global_device_ids=true, to_apply=%region_9.0 | all-reduce | flops 4 | bytes 32 | tf_op jit(solution)/shard_map/psum | solution.py:31
  78.3 12.5 %psum.37 = f32[4]{0:T(128)S(1)} all-reduce(f32[4]{0:T(128)S(1)} %psum.36), channel_id=1, replica_groups=mesh['row_0'=8,'row_1'=4,'col_0'=2,'col_1'=4,'col_2'=2] {'col_0'}, use_global_device_ids=true, to_apply=%region_10.0 | all-reduce | flops 4 | bytes 32 | tf_op jit(solution)/shard_map/psum | solution.py:31
  90.8 24.8 %psum.38 = f32[4]{0:T(128)S(1)} all-reduce(f32[4]{0:T(128)S(1)} %psum.37), channel_id=1, replica_groups=mesh['row_0'=8,'row_1'=4,'col_0'=2,'col_1'=4,'col_2'=2] {'col_1'}, use_global_device_ids=true, to_apply=%region_11.0 | all-reduce | flops 4 | bytes 32 | tf_op jit(solution)/shard_map/psum | solution.py:31
  115.6 2.5 %psum.39 = f32[4]{0:T(128)S(1)} all-reduce(f32[4]{0:T(128)S(1)} %psum.38), channel_id=1, replica_groups=mesh['row_0'=8,'row_1'=4,'col_0'=2,'col_1'=4,'col_2'=2] {'col_2'}, use_global_device_ids=true, to_apply=%region_12.0 | all-reduce | flops 4 | bytes 32 | tf_op jit(solution)/shard_map/psum | solution.py:31
  118.1 0.5 broadcast_multiply_fusion.5
  (29 shorter events, 1.1 us)
Async XLA Ops:
  0.6 8.1 %copy-start = (f32[32,2048]{1,0:T(8,128)S(1)}, f32[32,2048]{1,0:T(8,128)}, u32[]{:S(2)}) copy-start(f32[32,2048]{1,0:T(8,128)} %param.1) | copy-start | bytes 786436
  1.6 6.0 %collective-permute-start.1 = (f32[5,2048]{1,0:T(8,128)S(1)}, f32[5,2048]{1,0:T(8,128)S(1)}, u32[]{:S(2)}, u32[]{:S(2)}) collective-permute-start(f32[5,2048]{1,0:T(8,128)S(1)} %get-tuple-element.24), channel_id=1, source_target_pairs={{16,0},{32,16},{48,32},{64,48},{80,64},{96,80},{112,96},{128,112},... | collective-permute-start | bytes 122888 | tf_op jit(solution)/shard_map/ppermute | solution.py:24
  2.9 5.9 %collective-permute-start = (f32[5,2048]{1,0:T(8,128)S(1)}, f32[5,2048]{1,0:T(8,128)S(1)}, u32[]{:S(2)}, u32[]{:S(2)}) collective-permute-start(f32[5,2048]{1,0:T(8,128)S(1)} %get-tuple-element.23), channel_id=1, source_target_pairs={{0,16},{16,32},{32,48},{48,64},{64,80},{80,96},{96,112},{112,128},... | collective-permute-start | bytes 122888 | tf_op jit(solution)/shard_map/ppermute | solution.py:23
  8.9 10.7 %collective-permute-start.2 = (f32[42,5]{1,0:T(8,128)S(1)}, f32[42,5]{1,0:T(8,128)S(1)}, u32[]{:S(2)}, u32[]{:S(2)}) collective-permute-start(f32[42,5]{1,0:T(8,128)S(1)} %get-tuple-element.22), channel_id=1, source_target_pairs={{0,1},{1,2},{2,3},{3,4},{4,5},{5,6},{6,7},{7,8},{8,9},{9,10},{10,1... | collective-permute-start | bytes 2528 | tf_op jit(solution)/shard_map/ppermute | solution.py:23
  14.0 6.3 %collective-permute-start.3 = (f32[42,5]{1,0:T(8,128)S(1)}, f32[42,5]{1,0:T(8,128)S(1)}, u32[]{:S(2)}, u32[]{:S(2)}) collective-permute-start(f32[42,5]{1,0:T(8,128)S(1)} %get-tuple-element.21), channel_id=1, source_target_pairs={{1,0},{2,1},{3,2},{4,3},{5,4},{6,5},{7,6},{8,7},{9,8},{10,9},{11,1... | collective-permute-start | bytes 2528 | tf_op jit(solution)/shard_map/ppermute | solution.py:24
where the time goes:
time: 119 us
  blocking collectives  81.8 us (69%)
  starting transfers between devices  16.4 us (14%)
  other arithmetic  11 us (9%)
  between operations  6.05 us (5%)
  waiting for transfers between devices  1.83 us (2%)
  local copies, waits for them, and re-layouts  1.49 us (1%)
    psum x5, blocking collectives, by_axis(): shard = lax.psum(shard, axis)  81.8 us
    ppermute x2, starting transfers between devices, with_halo(): before = lax.ppermute(last, axis, up)  9.7 us
    ppermute x2, starting transfers between devices, with_halo(): after = lax.ppermute(first, axis, down)  6.75 us
  transfers between devices with their start and end apart: 4, of which 2 were waited for; matrix products, arithmetic and copies ran while one was open for 0% of the time, Pallas kernels for 0%

commit v1 on v0

--- a/solution.py
+++ b/solution.py
@@ -28,7 +28,7 @@
 
 def by_axis(shard, axes):
     for axis in axes:
-        shard = lax.psum(shard, axis)
+        shard = jnp.sum(lax.all_gather(shard, axis), axis=0)
     return shard
 
 

time: 119 us -> 124 us (1.042)
  local copies, waits for them, and re-layouts: 1.49 us -> 9.28 us
  blocking collectives: 81.8 us -> 76.5 us
  between operations: 6.05 us -> 9.36 us
    psum x5 -> x0, blocking collectives: 81.8 us -> none  [by_axis(): shard = lax.psum(shard, axis)]
    unnamed x0 -> x5, blocking collectives: none -> 76.5 us
    unnamed x2 -> x16, local copies, waits for them, and re-layouts: 0.01 us -> 7.38 us
  transfers between devices with their start and end apart: 4 -> 4, of which waited for: 2 -> 1; matrix products, arithmetic and copies ran while one was open for 0% -> 5% of each run, Pallas kernels for 0% -> 0%
where the time goes in v1:
time: 124 us
  blocking collectives  76.5 us (62%)
  starting transfers between devices  16.4 us (13%)
  other arithmetic  11.2 us (9%)
  between operations  9.36 us (8%)
  local copies, waits for them, and re-layouts  9.28 us (7%)
    unnamed x5, blocking collectives  76.5 us
    ppermute x2, starting transfers between devices, with_halo(): before = lax.ppermute(last, axis, up)  9.7 us
    unnamed x16, local copies, waits for them, and re-layouts  7.38 us
    ppermute x2, starting transfers between devices, with_halo(): after = lax.ppermute(first, axis, down)  6.75 us
  transfers between devices with their start and end apart: 4, of which 1 were waited for; matrix products, arithmetic and copies ran while one was open for 5% of the time, Pallas kernels for 0%

profile of v1, /device:TPU:1, one launch (start us, length us, event | category | flops | bytes accessed | tf_op | source)
XLA Modules:
  0.0 123.8 jit_solution(707944269575873974)
XLA Ops:
  0.6 0.9 fusion.92
  1.6 1.3 %collective-permute-start.1 = (f32[5,2048]{1,0:T(8,128)S(1)}, f32[5,2048]{1,0:T(8,128)S(1)}, u32[]{:S(2)}, u32[]{:S(2)}) collective-permute-start(f32[5,2048]{1,0:T(8,128)S(1)} %get-tuple-element.24), channel_id=1, source_target_pairs={{16,0},{32,16},{48,32},{64,48},{80,64},{96,80},{112,96},{128,112},... | collective-permute-start | bytes 122888 | tf_op jit(solution)/shard_map/ppermute | solution.py:24
  2.9 4.6 %collective-permute-start = (f32[5,2048]{1,0:T(8,128)S(1)}, f32[5,2048]{1,0:T(8,128)S(1)}, u32[]{:S(2)}, u32[]{:S(2)}) collective-permute-start(f32[5,2048]{1,0:T(8,128)S(1)} %get-tuple-element.23), channel_id=1, source_target_pairs={{0,16},{16,32},{32,48},{48,64},{64,80},{80,96},{96,112},{112,128},... | collective-permute-start | bytes 122888 | tf_op jit(solution)/shard_map/ppermute | solution.py:23
  7.5 0.1 broadcast_and_fusion
  7.8 1.0 collective-permute-done
  8.9 5.1 %collective-permute-start.2 = (f32[42,5]{1,0:T(8,128)S(1)}, f32[42,5]{1,0:T(8,128)S(1)}, u32[]{:S(2)}, u32[]{:S(2)}) collective-permute-start(f32[42,5]{1,0:T(8,128)S(1)} %get-tuple-element.22), channel_id=1, source_target_pairs={{0,1},{1,2},{2,3},{3,4},{4,5},{5,6},{6,7},{7,8},{8,9},{9,10},{10,1... | collective-permute-start | bytes 2528 | tf_op jit(solution)/shard_map/ppermute | solution.py:23
  14.0 5.5 %collective-permute-start.3 = (f32[42,5]{1,0:T(8,128)S(1)}, f32[42,5]{1,0:T(8,128)S(1)}, u32[]{:S(2)}, u32[]{:S(2)}) collective-permute-start(f32[42,5]{1,0:T(8,128)S(1)} %get-tuple-element.21), channel_id=1, source_target_pairs={{1,0},{2,1},{3,2},{4,3},{5,4},{6,5},{7,6},{8,7},{9,8},{10,9},{11,1... | collective-permute-start | bytes 2528 | tf_op jit(solution)/shard_map/ppermute | solution.py:24
  19.5 1.3 %dynamic-slice = u32[1]{0:T(128)} dynamic-slice(u32[512]{0:T(512)} %constant.145, u32[]{:T(128)S(6)} %add.236), dynamic_slice_sizes={1} | dynamic-slice | bytes 12
  20.8 1.3 %dynamic-slice.1 = u32[1]{0:T(128)} dynamic-slice(u32[512]{0:T(512)} %constant.150, u32[]{:T(128)S(6)} %add.236), dynamic_slice_sizes={1} | dynamic-slice | bytes 12
  23.3 1.3 %dynamic-slice.2 = u32[1]{0:T(128)} dynamic-slice(u32[512]{0:T(512)} %constant.155, u32[]{:T(128)S(6)} %add.236), dynamic_slice_sizes={1} | dynamic-slice | bytes 12
  25.2 1.3 %dynamic-slice.3 = u32[1]{0:T(128)} dynamic-slice(u32[512]{0:T(512)} %constant.160, u32[]{:T(128)S(6)} %add.236), dynamic_slice_sizes={1} | dynamic-slice | bytes 12
  27.2 1.3 %dynamic-slice.4 = u32[1]{0:T(128)} dynamic-slice(u32[512]{0:T(512)} %constant.165, u32[]{:T(128)S(6)} %add.236), dynamic_slice_sizes={1} | dynamic-slice | bytes 12
  28.5 0.3 concatenate.79
  28.8 0.2 slice_subtract_fusion.14
  29.4 0.2 fusion.45
  29.7 0.2 fusion.46
  30.0 0.2 slice_subtract_fusion.12
  30.5 0.1 fusion
  30.7 0.2 fusion.36
  30.8 0.2 broadcast_multiply_fusion.2
  31.1 0.3 multiply_subtract_fusion.2
  31.4 0.2 slice_subtract_fusion.10
  31.9 0.2 fusion.1
  32.1 0.2 fusion.28
  32.3 0.3 broadcast_multiply_fusion.1
  32.7 0.4 multiply_subtract_fusion.1
  33.0 0.2 slice_subtract_fusion.8
  33.5 0.3 fusion.2
  33.8 0.2 fusion.20
  34.0 0.4 broadcast_multiply_fusion
  34.4 0.2 slice_subtract_fusion.6
  34.7 0.2 slice_subtract_fusion.4
  34.9 0.3 add_multiply_fusion
  35.2 0.2 slice_subtract_fusion.2
  35.5 0.2 slice_subtract_fusion
  35.7 2.0 %fusion.76 = (f32[]{:T(128)}, f32[]{:T(128)}, f32[]{:T(128)}, f32[]{:T(128)}, f32[32,2048]{1,0:T(8,128)}) fusion(f32[32,2048]{1,0:T(8,128)S(1)} %copy-done, f32[42,2058]{1,0:T(8,128)S(1)} %get-tuple-element.11, f32[42,2058]{1,0:T(8,128)S(1)} %get-tuple-element.12, f32[42,2058]{1,0:T(8,128)S(1)} %get-tuple-element.20, f32[42,2058]{1,0:T(8,128)S(1)} %get-tuple-element.18, ...), kind=kLoop, calls=%fused_computation.149 | loop fusion | flops 2359292 | bytes 2621456 | tf_op jit(solution)/shard_map/reduce_sum | solution.py:36
  37.7 1.6 %fusion.80 = (f32[]{:T(128)}, f32[]{:T(128)}, f32[]{:T(128)}, f32[]{:T(128)}) fusion(f32[42,2057]{1,0:T(8,128)S(1)} %slice_subtract_fusion.6, f32[41,2058]{1,0:T(8,128)S(1)} %slice_subtract_fusion.7, pred[42,2058]{1,0:T(8,128)(4,1)S(1)} %broadcast_and_fusion, pred[42,2058]{1,0:T(8,128)(4,1)S(1)} %broadcast_and_fusion.1, ...), kind=kLoop, calls=%fused_computation.154 | loop fusion | flops 1572860 | bytes 2863440 | tf_op jit(solution)/shard_map/reduce_sum | solution.py:36
  44.4 0.2 maximum_dynamic-update-slice_fusion
  44.6 33.8 %all-reduce.24 = f32[32]{0:T(128)S(1)} all-reduce(f32[32]{0:T(128)S(1)} %maximum_dynamic-update-slice_fusion), channel_id=2, replica_groups=mesh['row_0'=8,'row_1'=4,'col_0'=2,'col_1'=4,'col_2'=2] {'row_0'}, use_global_device_ids=true, to_apply=%add.24 | all-reduce | flops 32 | bytes 256
  78.5 0.2 dynamic-update-slice.1
  78.7 6.0 %all-reduce.25 = f32[16]{0:T(128)S(1)} all-reduce(f32[16]{0:T(128)S(1)} %dynamic-update-slice.1), channel_id=3, replica_groups=mesh['row_0'=8,'row_1'=4,'col_0'=2,'col_1'=4,'col_2'=2] {'row_1'}, use_global_device_ids=true, to_apply=%add.25 | all-reduce | flops 16 | bytes 128
  84.8 0.2 dynamic-update-slice.2
  85.7 12.5 %all-reduce.26 = f32[8]{0:T(128)S(1)} all-reduce(f32[8]{0:T(128)S(1)} %dynamic-update-slice.2), channel_id=4, replica_groups=mesh['row_0'=8,'row_1'=4,'col_0'=2,'col_1'=4,'col_2'=2] {'col_0'}, use_global_device_ids=true, to_apply=%add.26 | all-reduce | flops 8 | bytes 64
  98.3 0.2 dynamic-update-slice.3
  98.5 18.9 %all-reduce.27 = f32[16]{0:T(128)S(1)} all-reduce(f32[16]{0:T(128)S(1)} %dynamic-update-slice.3), channel_id=5, replica_groups=mesh['row_0'=8,'row_1'=4,'col_0'=2,'col_1'=4,'col_2'=2] {'col_1'}, use_global_device_ids=true, to_apply=%add.27 | all-reduce | flops 16 | bytes 128
  117.6 0.2 dynamic-update-slice.4
  117.8 5.3 %all-reduce.28 = f32[8]{0:T(128)S(1)} all-reduce(f32[8]{0:T(128)S(1)} %dynamic-update-slice.4), channel_id=6, replica_groups=mesh['row_0'=8,'row_1'=4,'col_0'=2,'col_1'=4,'col_2'=2] {'col_2'}, use_global_device_ids=true, to_apply=%add.28 | all-reduce | flops 8 | bytes 64
  123.3 0.5 broadcast_multiply_fusion.5
  (53 shorter events, 2.6 us)
Async XLA Ops:
  0.6 8.1 %copy-start = (f32[32,2048]{1,0:T(8,128)S(1)}, f32[32,2048]{1,0:T(8,128)}, u32[]{:S(2)}) copy-start(f32[32,2048]{1,0:T(8,128)} %param.1) | copy-start | bytes 786436
  1.6 6.2 %collective-permute-start.1 = (f32[5,2048]{1,0:T(8,128)S(1)}, f32[5,2048]{1,0:T(8,128)S(1)}, u32[]{:S(2)}, u32[]{:S(2)}) collective-permute-start(f32[5,2048]{1,0:T(8,128)S(1)} %get-tuple-element.24), channel_id=1, source_target_pairs={{16,0},{32,16},{48,32},{64,48},{80,64},{96,80},{112,96},{128,112},... | collective-permute-start | bytes 122888 | tf_op jit(solution)/shard_map/ppermute | solution.py:24
  2.9 5.9 %collective-permute-start = (f32[5,2048]{1,0:T(8,128)S(1)}, f32[5,2048]{1,0:T(8,128)S(1)}, u32[]{:S(2)}, u32[]{:S(2)}) collective-permute-start(f32[5,2048]{1,0:T(8,128)S(1)} %get-tuple-element.23), channel_id=1, source_target_pairs={{0,16},{16,32},{32,48},{48,64},{64,80},{80,96},{96,112},{112,128},... | collective-permute-start | bytes 122888 | tf_op jit(solution)/shard_map/ppermute | solution.py:23
  8.9 19.6 %collective-permute-start.2 = (f32[42,5]{1,0:T(8,128)S(1)}, f32[42,5]{1,0:T(8,128)S(1)}, u32[]{:S(2)}, u32[]{:S(2)}) collective-permute-start(f32[42,5]{1,0:T(8,128)S(1)} %get-tuple-element.22), channel_id=1, source_target_pairs={{0,1},{1,2},{2,3},{3,4},{4,5},{5,6},{6,7},{7,8},{8,9},{9,10},{10,1... | collective-permute-start | bytes 2528 | tf_op jit(solution)/shard_map/ppermute | solution.py:23
  14.0 14.5 %collective-permute-start.3 = (f32[42,5]{1,0:T(8,128)S(1)}, f32[42,5]{1,0:T(8,128)S(1)}, u32[]{:S(2)}, u32[]{:S(2)}) collective-permute-start(f32[42,5]{1,0:T(8,128)S(1)} %get-tuple-element.21), channel_id=1, source_target_pairs={{1,0},{2,1},{3,2},{4,3},{5,4},{6,5},{7,6},{8,7},{9,8},{10,9},{11,1... | collective-permute-start | bytes 2528 | tf_op jit(solution)/shard_map/ppermute | solution.py:24
